TPU v7x, 128 devices: a whole 4x4x4 slice. The times are simulated.
128 devices in a mesh: samp: 16 (over z, y_lo, core), var: 8 (over x, y_hi).
Axes of the slice: x: 4, y: 4 (y_hi: 2, y_lo: 2; y = y_hi * 2 + y_lo), z: 4, core: 2. Of those that a mesh axis runs over, the one named last changes fastest.
Arguments:
- hap_words: int32 [2, 1024, 1024], P(None, 'samp', 'var'), may hold values from 0 to 1073741823
- total_counts: int32 [30720, 8192], P('samp', 'var'), may hold values from 0 to 4999
- allele_one: int32 [30720, 8192], P('samp', 'var'), may hold values from 0 to 299
- allele_two: int32 [30720, 8192], P('samp', 'var'), may hold values from 0 to 299
Outputs:
- z_total: float32 [1024, 8192], P('samp', 'var')
- z_allelic: float32 [1024, 8192], P('samp', 'var')
Inputs may be any that keep to these rules, and one draw needn't show every extreme that they name: Bit k, for k below 30, of hap_words[c, j, v] is haplotype c of sample 30 * j + k at variant v; higher bits are zero.
All inputs are finite; a program needn't handle non-finite values.
Results may differ from a plain program's by a relative error of at most 0.0003.
The roundings to bfloat16 on the way count: a program that leaves them out, or rounds other values in their place, can miss the bound.
Values sent between devices are 32-bit elements; how exact they have to be, the bound alone decides.
A program may use at most 192 MiB of HBM per device.

v0:
```python
import jax
import jax.numpy as jnp
from jax import lax
from jax.sharding import PartitionSpec as P

BITS = 30


def from_everyone(shard, axis):
    copies = jnp.broadcast_to(shard, (lax.axis_size(axis), *shard.shape))
    return lax.all_to_all(copies, axis, split_axis=0, concat_axis=0, tiled=True)


def joined_along(tiles, dim):
    tiles = jnp.moveaxis(tiles, 0, dim)
    dims = tiles.shape
    return tiles.reshape(*dims[:dim], dims[dim] * dims[dim + 1], *dims[dim + 2 :])


def collect(shard, axis, dim):
    tiles = from_everyone(shard, axis)
    return joined_along(tiles, dim)


def of_everyone(shard, axis):
    return from_everyone(shard, axis).sum(axis=0)


def unpack(packed):
    shifts = jnp.arange(BITS, dtype=jnp.int32)
    bit_table = jnp.bitwise_and(
        jnp.right_shift(packed[:, :, None, :], shifts[None, None, :, None]), 1
    )
    return bit_table.reshape(2, packed.shape[1] * BITS, packed.shape[2])


def features(total_part, one_part, two_part):
    log_total = jnp.log1p(total_part.astype(jnp.float32))
    one_plus = one_part.astype(jnp.float32) + 1.0
    two_plus = two_part.astype(jnp.float32) + 1.0
    log_ratio = jnp.log(one_plus / two_plus)
    weight = 1.0 / (1.0 / one_plus + 1.0 / two_plus)
    return (log_total, (weight * log_ratio).astype(jnp.bfloat16), weight.astype(jnp.bfloat16))


def finish(pair_sums, dos_margin, gene_margin, sample_count):
    dos_sum, dos_sq = (dos_margin[0], dos_margin[1])
    gene_sum, gene_sq = (gene_margin[0], gene_margin[1])
    dosage_var = dos_sq - dos_sum * dos_sum / sample_count
    gene_var = gene_sq - gene_sum * gene_sum / sample_count
    covariance = pair_sums[0] - dos_sum[:, None] * gene_sum[None, :] / sample_count
    z_total = (
        jnp.sqrt(sample_count)
        * covariance
        / jnp.sqrt((dosage_var[:, None] + 1.0) * (gene_var[None, :] + 1.0))
    )
    z_allelic = pair_sums[1] / jnp.sqrt(pair_sums[2] + 1.0)
    return (z_total, z_allelic)


def per_device(hap_words, total_counts, allele_one, allele_two):
    panel_words = collect(hap_words, "var", 2)
    bit_table = unpack(panel_words)
    dosage_b = (bit_table[0] + bit_table[1] - 1).astype(jnp.bfloat16)
    phase_int = bit_table[0] - bit_table[1]
    phase_b = phase_int.astype(jnp.bfloat16)
    phase_sq_b = (phase_int * phase_int).astype(jnp.bfloat16)
    dos_margin = jnp.stack(
        [
            jnp.sum(dosage_b, axis=0, dtype=jnp.float32),
            jnp.sum(dosage_b * dosage_b, axis=0, dtype=jnp.float32),
        ]
    )
    log_total, weighted_b, weight_b = features(total_counts, allele_one, allele_two)
    gene_margin = jnp.stack([jnp.sum(log_total, axis=0), jnp.sum(log_total * log_total, axis=0)])
    cross_total = jnp.einsum(
        "sv,sg->vg", dosage_b, log_total.astype(jnp.bfloat16), preferred_element_type=jnp.float32
    )
    cross_allelic = jnp.einsum("sv,sg->vg", phase_b, weighted_b, preferred_element_type=jnp.float32)
    het_weight = jnp.einsum("sv,sg->vg", phase_sq_b, weight_b, preferred_element_type=jnp.float32)
    pair_sums = jnp.stack([cross_total, cross_allelic, het_weight])
    sample_groups = lax.axis_size("samp")
    sample_count = jnp.float32(bit_table.shape[1] * sample_groups)
    own_pairs, own_dos = (
        lax.psum_scatter(pair_sums, "samp", scatter_dimension=1, tiled=True),
        lax.psum_scatter(dos_margin, "samp", scatter_dimension=1, tiled=True),
    )
    summed_genes = of_everyone(gene_margin, "samp")
    return finish(own_pairs, own_dos, summed_genes, sample_count)


def solution(mesh):
    in_specs = (P(None, "samp", "var"), P("samp", "var"), P("samp", "var"), P("samp", "var"))
    out_specs = (P("samp", "var"), P("samp", "var"))
    return jax.shard_map(
        per_device, mesh=mesh, in_specs=in_specs, out_specs=out_specs, check_vma=False
    )
```

profile of v0, /device:TPU:1, one launch (start us, length us, event | category | flops | bytes accessed | tf_op | source)
XLA Modules:
  0.0 249.5 jit_solution(4785275044413136693)
XLA Ops:
  7.2 0.0 reduce-scatter.7.cloned.1.call-start
  7.2 0.9 broadcast_in_dim.4
  8.1 17.0 %all_to_all.10 = s32[8,2,64,128]{3,2,1,0:T(8,128)S(1)} all-to-all(s32[8,2,64,128]{3,2,1,0:T(8,128)S(1)} %broadcast_in_dim.4), channel_id=1, replica_groups=mesh['samp'=16,'var'=8] {'var'}, dimensions={0} | all-to-all | bytes 1048576 | tf_op jit(solution)/shard_map/all_to_all | solution.py:11
  25.2 2.7 %shift-right-arithmetic_and_fusion = s32[2,64,30,1024]{3,2,1,0:T(8,128)S(1)} fusion(s32[2,64,1024]{2,1,0:T(8,128)S(1)} %copy_bitcast_fusion), kind=kLoop, calls=%fused_computation | loop fusion | flops 7864320 | bytes 16252928 | tf_op jit(solution)/shard_map/and | solution.py:31
  27.9 4.1 %convert_reduce_fusion.1 = (f32[1024]{0:T(1024)S(1)}, f32[1024]{0:T(1024)S(1)}, bf16[1,64,30,1024]{3,2,1,0:T(8,128)(2,1)}) fusion(s32[2,64,30,1024]{3,2,1,0:T(8,128)S(1)} %shift-right-arithmetic_and_fusion), kind=kLoop, calls=%fused_computation.3 | loop fusion | flops 15726592 | bytes 19668992 | tf_op jit(solution)/shard_map/reduce_sum | solution.py:70
  32.0 4.7 %fusion.7 = (bf16[1,64,30,1024]{3,2,1,0:T(8,128)(2,1)}, bf16[1,64,30,1024]{3,2,1,0:T(8,128)(2,1)}) fusion(s32[2,64,30,1024]{3,2,1,0:T(8,128)S(1)} %shift-right-arithmetic_and_fusion), kind=kLoop, calls=%fused_computation.19 | loop fusion | flops 7864320 | bytes 23592960 | tf_op jit(solution)/shard_map/convert_element_type | solution.py:66
  36.6 1.0 copy.10
  37.7 0.0 reduce-scatter.7.cloned.1.call-update
  37.7 0.2 reduce-scatter.5.cloned.1.call-start
  37.9 6.1 %convert_element_type.47 = bf16[1920,1024]{1,0:T(8,128)(2,1)} reshape(bf16[1,64,30,1024]{3,2,1,0:T(8,128)(2,1)} %get-tuple-element.6) | data formatting | bytes 7864320 | tf_op jit(solution)/shard_map/convert_element_type | solution.py:64
  44.1 6.0 %convert_element_type.51 = bf16[1920,1024]{1,0:T(8,128)(2,1)} reshape(bf16[1,64,30,1024]{3,2,1,0:T(8,128)(2,1)} %get-tuple-element.7) | data formatting | bytes 7864320 | tf_op jit(solution)/shard_map/convert_element_type | solution.py:66
  50.1 6.1 %convert_element_type.56 = bf16[1920,1024]{1,0:T(8,128)(2,1)} reshape(bf16[1,64,30,1024]{3,2,1,0:T(8,128)(2,1)} %get-tuple-element.8) | data formatting | bytes 7864320 | tf_op jit(solution)/shard_map/convert_element_type | solution.py:67
  56.2 0.0 copy-start.1
  56.2 9.8 %fusion.8 = f32[1,1024,1024]{2,1,0:T(8,128)S(1)} fusion(bf16[1920,1024]{1,0:T(8,128)(2,1)} %convert_element_type.51, s32[1920,1024]{1,0:T(8,128)} %param.6, s32[1920,1024]{1,0:T(8,128)} %param.7), kind=kOutput, calls=%fused_computation.20 | convolution fusion | flops 4048158720 | bytes 23855104 | tf_op jit(solution)/shard_map/sv,sg->vg/dot_general | solution.py:79
  66.0 0.0 copy-done.1
  66.0 0.0 copy-start
  66.0 8.6 %fusion.9 = f32[1,1024,1024]{2,1,0:T(8,128)S(1)} fusion(bf16[1920,1024]{1,0:T(8,128)(2,1)S(1)} %copy-done.1, s32[1920,1024]{1,0:T(8,128)} %param.6, s32[1920,1024]{1,0:T(8,128)} %param.7), kind=kOutput, calls=%fused_computation.21 | convolution fusion | flops 4044226560 | bytes 23855104 | tf_op jit(solution)/shard_map/sv,sg->vg/dot_general | solution.py:80
  74.6 0.0 copy-done
  74.6 7.2 %fusion.12 = f32[1,1024,1024]{2,1,0:T(8,128)S(1)} fusion(bf16[1920,1024]{1,0:T(8,128)(2,1)S(1)} %copy-done, s32[1920,1024]{1,0:T(8,128)} %param.5), kind=kOutput, calls=%fused_computation.22 | convolution fusion | flops 4030464000 | bytes 15990784 | tf_op jit(solution)/shard_map/sv,sg->vg/dot_general | solution.py:76
  81.8 5.3 %pad_maximum_fusion = f32[3,1024,1024]{2,1,0:T(8,128)} fusion(f32[1,1024,1024]{2,1,0:T(8,128)S(1)} %fusion.9, f32[1,1024,1024]{2,1,0:T(8,128)S(1)} %fusion.8, f32[1,1024,1024]{2,1,0:T(8,128)S(1)} %fusion.12), kind=kLoop, calls=%fused_computation.1 | loop fusion | flops 6291456 | bytes 25165824 | tf_op jit(solution)/shard_map/stack | solution.py:81
  87.1 0.0 reduce-scatter.5.cloned.1.call-update
  87.1 6.6 %fusion = (f32[1024]{0:T(1024)S(1)}, f32[1024]{0:T(1024)S(1)}) fusion(s32[1920,1024]{1,0:T(8,128)} %param.5), kind=kLoop, calls=%fused_computation.13 | loop fusion | flops 7862272 | bytes 7872512 | tf_op jit(solution)/shard_map/reduce_sum | solution.py:75
  93.8 13.8 %all_to_all.11 = f32[16,2,1024]{2,1,0:T(2,128)S(1)} all-to-all(f32[16,2,1024]{2,1,0:T(2,128)S(1)} %broadcast_in_dim.10), channel_id=1, replica_groups=mesh['samp'=16,'var'=8] {'samp'}, dimensions={0} | all-to-all | bytes 262144 | tf_op jit(solution)/shard_map/all_to_all | solution.py:11
  107.6 0.1 reduce_sum.49
  107.6 0.0 reduce-scatter.7.cloned.1.call-done
  107.7 0.9 fusion.24
  108.6 0.1 copy.13
  108.6 0.1 copy.15
  108.7 130.4 %reduce-scatter.5.cloned.1.call-done = f32[3,64,1024]{2,1,0:T(8,128)} async-done(((f32[3,1024,1024]{2,1,0:T(8,128)}), f32[3,64,1024]{2,1,0:T(8,128)}) %reduce-scatter.5.cloned.1.call-update) | async-done | bytes 786448 | tf_op jit(solution)/shard_map/reduce_scatter | solution.py:85
  239.1 1.8 fusion.17
  240.9 1.8 fusion.20
  (6 shorter events, 0.1 us)
Async XLA Ops:
  7.2 100.5 %reduce-scatter.7.cloned.1.call-start = ((), (), s32[]{:S(2)}) async-start(), calls=%async_computation.5 | async-start | bytes 557056
  37.7 201.4 %reduce-scatter.5.cloned.1.call-start = ((), (), s32[]{:S(2)}) async-start(), calls=%async_computation.4 | async-start | bytes 13369344 | tf_op jit(solution)/shard_map/reduce_scatter | solution.py:85
  56.2 9.8 %copy-start.1 = (bf16[1920,1024]{1,0:T(8,128)(2,1)S(1)}, bf16[1920,1024]{1,0:T(8,128)(2,1)}, u32[]{:S(2)}) copy-start(bf16[1920,1024]{1,0:T(8,128)(2,1)} %convert_element_type.56) | copy-start | bytes 11796484
  66.0 8.6 %copy-start = (bf16[1920,1024]{1,0:T(8,128)(2,1)S(1)}, bf16[1920,1024]{1,0:T(8,128)(2,1)}, u32[]{:S(2)}) copy-start(bf16[1920,1024]{1,0:T(8,128)(2,1)} %convert_element_type.47) | copy-start | bytes 11796484
Sparse Core Ops, SparseCore 0:
  37.8 58.2 reduce-scatter.6
  98.5 140.4 reduce-scatter.4
where the time goes:
time: 251 us; the launch traced here: 249 us
  waiting for transfers between devices  130 us (52%)
  blocking collectives  30.8 us (12%)
  other arithmetic  27 us (11%)
  matrix products  25.6 us (10%)
  local copies, waits for them, and re-layouts  21.3 us (8%)
  between operations  14.1 us (6%)
    reduce_scatter x1, waiting for transfers between devices, per_device(): lax.psum_scatter(pair_sums, 'samp', scatter_dimension=1, tiled=True)  130 us
    all_to_all x2, blocking collectives, from_everyone(): return lax.all_to_all(copies, axis, split_axis=0, concat_axis=0, tiled=True)  30.8 us
    dot_general x1, matrix products, per_device(): jnp.einsum('sv,sg->vg', phase_b, weighted_b, preferred_element_type=jnp.f...  9.8 us
    dot_general x1, matrix products, per_device(): jnp.einsum('sv,sg->vg', phase_sq_b, weight_b, preferred_element_type=jnp....  8.59 us
    dot_general x1, matrix products, per_device(): jnp.einsum('sv,sg->vg', dosage_b, log_total.astype(jnp.bfloat16), preferr...  7.16 us
    reduce_sum x1, other arithmetic, per_device(): jnp.sum(log_total, axis=0)  6.57 us
    convert_element_type x1, local copies, waits for them, and re-layouts, per_device(): dosage_b = (bit_table[0] + bit_table[1] - 1).astype(jnp.bfloat16)  6.14 us
    convert_element_type x1, local copies, waits for them, and re-layouts, per_device(): phase_sq_b = (phase_int * phase_int).astype(jnp.bfloat16)  6.09 us
  transfers between devices with their start and end apart: 2, of which 1 were waited for; matrix products, arithmetic and copies ran while one was open for 23% of the time, Pallas kernels for 0%

commit v1 on v0

v1 whole, which is shorter than its diff:
```python
import functools

import jax
import jax.numpy as jnp
from jax import lax
from jax.experimental import pallas as pl
from jax.experimental.pallas import tpu as pltpu
from jax.sharding import PartitionSpec as P

BITS = 30
ROWS_IN = 128
SLOTS = 4
LANES = 256
MESH = pl.DeviceIdType.MESH
BF16 = jnp.bfloat16
F32 = jnp.float32


def kernel(
    n_var,
    sample_count,
    hap_ref,
    total_ref,
    one_ref,
    two_ref,
    zt_ref,
    za_ref,
    hall,
    feats,
    counts,
    gacc,
    tbuf,
    lhs,
    acc,
    r0,
    r1,
    r2,
    r3,
    marg,
    mrecv,
    in_sem,
    hap_own,
    hap_send,
    hap_recv,
    s0s,
    s0r,
    s1s,
    s1r,
    s2s,
    s2r,
    s3s,
    s3r,
    ms,
    mr,
):
    samples, genes = total_ref.shape
    words = hap_ref.shape[1]
    rows = acc.shape[4]
    s = lax.axis_index("samp")
    v = lax.axis_index("var")
    c = s % 2
    y = (s // 2) % 2
    z = s // 4
    za = z + 1 - 2 * (z % 2)
    zb = 3 - z
    zc = (z + 2) % 4
    core_dev = (s + 1 - 2 * c, v)
    y_dev = (s + 2 - 4 * y, v)
    a_dev = (za * 4 + y * 2 + c, v)
    b_dev = (zb * 4 + y * 2 + c, v)
    cube = (core_dev, y_dev, a_dev, b_dev)
    oc = 1 - c
    oy = 1 - y

    n_chunks = samples // ROWS_IN

    def fetch(k, slot, which, ref):
        return pltpu.make_async_copy(
            ref.at[pl.ds(pl.multiple_of(k * ROWS_IN, ROWS_IN), ROWS_IN), :],
            counts.at[slot, which],
            in_sem.at[slot, which],
        )

    sources = (total_ref, one_ref, two_ref)
    for k in range(SLOTS - 1):
        for which, ref in enumerate(sources):
            fetch(k, k, which, ref).start()

    barrier = pltpu.get_barrier_semaphore()
    for dev in cube:
        pl.semaphore_signal(barrier, inc=1, device_id=dev, device_id_type=MESH)
    for k in range(1, n_var):
        pl.semaphore_signal(
            barrier, inc=1, device_id=(s, (v + k) % n_var), device_id_type=MESH
        )
    pl.semaphore_wait(barrier, 4 + n_var - 1)

    own = pltpu.make_async_copy(hap_ref, hall.at[v], hap_own)
    own.start()

    def hap_copy(k):
        return pltpu.make_async_remote_copy(
            src_ref=hap_ref,
            dst_ref=hall.at[v],
            send_sem=hap_send.at[k],
            recv_sem=hap_recv.at[k],
            device_id=(s, (v + k) % n_var),
            device_id_type=MESH,
        )

    def hap_arrival(k):
        return pltpu.make_async_remote_copy(
            src_ref=hap_ref,
            dst_ref=hall.at[(v + n_var - k) % n_var],
            send_sem=hap_send.at[k],
            recv_sem=hap_recv.at[k],
            device_id=(s, (v + k) % n_var),
            device_id_type=MESH,
        )

    for k in range(1, n_var):
        hap_copy(k).start()

    gacc[...] = jnp.zeros_like(gacc)

    def chunk_step(k, carry):
        slot = k % SLOTS

        @pl.when(k + SLOTS - 1 < n_chunks)
        def _():
            for which, ref in enumerate(sources):
                fetch(k + SLOTS - 1, (k + SLOTS - 1) % SLOTS, which, ref).start()

        for which, ref in enumerate(sources):
            fetch(k, slot, which, ref).wait()

        def row_step(r, carry):
            at = pl.ds(pl.multiple_of(r * 16, 16), 16)
            out = pl.ds(pl.multiple_of(k * ROWS_IN + r * 16, 16), 16)
            for lane in range(0, genes, LANES):
                cols = pl.ds(lane, LANES)
                log_total = jnp.log((counts[slot, 0, at, cols] + 1).astype(F32))
                one = (counts[slot, 1, at, cols] + 1).astype(F32)
                two = (counts[slot, 2, at, cols] + 1).astype(F32)
                weight = (one * two) / (one + two)
                weighted = weight * (jnp.log(one) - jnp.log(two))
                feats[0, out, cols] = log_total.astype(BF16)
                feats[1, out, cols] = weighted.astype(BF16)
                feats[2, out, cols] = weight.astype(BF16)
                square = log_total * log_total
                gacc[0, :, cols] += log_total[:8] + log_total[8:]
                gacc[1, :, cols] += square[:8] + square[8:]
            return carry

        lax.fori_loop(0, ROWS_IN // 16, row_step, 0)
        return carry

    lax.fori_loop(0, n_chunks, chunk_step, 0)

    own.wait()
    for k in range(1, n_var):
        hap_arrival(k).wait_recv()

    marg[0] = jnp.zeros_like(marg[0])
    marg[0, 0:1, :] = jnp.sum(gacc[0], axis=0, keepdims=True)
    marg[0, 1:2, :] = jnp.sum(gacc[1], axis=0, keepdims=True)
    for b in range(n_var):
        w0, w1 = hall[b, 0], hall[b, 1]
        bits = lax.population_count(w0) + lax.population_count(w1)
        het = lax.population_count(jnp.bitwise_xor(w0, w1))
        cols = pl.ds(b * 128, 128)
        bit_sum = jnp.sum(bits.astype(F32), axis=0, keepdims=True)
        het_sum = jnp.sum(het.astype(F32), axis=0, keepdims=True)
        marg[0, 2:3, cols] = bit_sum - float(samples)
        marg[0, 3:4, cols] = float(samples) - het_sum

    def marg_copy(k):
        return pltpu.make_async_remote_copy(
            src_ref=marg.at[k],
            dst_ref=mrecv.at[k],
            send_sem=ms.at[k],
            recv_sem=mr.at[k],
            device_id=cube[k],
            device_id_type=MESH,
        )

    def marg_finish(k):
        marg_copy(k).wait_recv()
        marg[k + 1] = marg[k] + mrecv[k]

    marg_copy(0).start()

    def send(src, dst, ss, rs, dev):
        return pltpu.make_async_remote_copy(
            src_ref=src,
            dst_ref=dst,
            send_sem=ss,
            recv_sem=rs,
            device_id=dev,
            device_id_type=MESH,
        )

    def s0(p, i, t):
        return send(acc.at[p, i, t, oc], r0.at[p, i, t], s0s.at[p, i, t], s0r.at[p, i, t], core_dev)

    def s0_finish(p, i):
        for t in range(2):
            s0(p, i, t).wait_recv()
            acc[p, i, t, c] = acc[p, i, t, c] + r0[p, i, t]

    def s1_total(i):
        return send(acc.at[0, i, oy, c], r1.at[0, i], s1s.at[0, i], s1r.at[0, i], y_dev)

    def s1_allelic(i, t):
        at = 2 * i + t
        return send(acc.at[1, i, t, c], r1.at[1, at], s1s.at[1, at], s1r.at[1, at], a_dev)

    def s1_het(i, t):
        return send(acc.at[2, i, t, c], r1.at[2, i + t], s1s.at[2, i + t], s1r.at[2, i + t], b_dev)

    def s0_then_s1(p, i):
        s0_finish(p, i)
        if p == 0:
            s1_total(i).start()
        elif p == 1:

            @pl.when(i < 2)
            def _():
                for t in range(2):
                    s1_allelic(i, t).start()
        else:

            @pl.when(i % 2 == 0)
            def _():
                for t in range(2):
                    s1_het(i, t).start()

    iota = lax.broadcasted_iota(jnp.int32, (8, 128), 0)

    def unpack(i):
        zt = jnp.where(i == 0, zc, jnp.where(i == 1, za, jnp.where(i == 2, zb, z)))
        for b in range(2):
            block = 2 * zt + b

            def word_step(g, carry):
                at = pl.ds(pl.multiple_of(g * 8, 8), 8)
                w0 = hall[block, 0, at, :]
                w1 = hall[block, 1, at, :] << 1
                parts = []
                for t in range(BITS):
                    first = 8 * t // BITS
                    last = (8 * t + 7) // BITS
                    shift = iota + (8 * t - BITS * first)
                    u0 = jnp.broadcast_to(w0[first : first + 1], (8, 128))
                    u1 = jnp.broadcast_to(w1[first : first + 1], (8, 128))
                    if last != first:
                        early = iota < BITS * last - 8 * t
                        shift = jnp.where(early, shift, shift - BITS)
                        u0 = jnp.where(early, u0, jnp.broadcast_to(w0[last : last + 1], (8, 128)))
                        u1 = jnp.where(early, u1, jnp.broadcast_to(w1[last : last + 1], (8, 128)))
                    code = ((u0 >> shift) & 1) | ((u1 >> shift) & 2)
                    parts.append(code.astype(F32))
                out = pl.ds(pl.multiple_of(g * 8 * BITS, 16), 8 * BITS)
                tbuf[out, :] = jnp.concatenate(parts, axis=0).astype(BF16)
                return carry

            lax.fori_loop(0, words // 8, word_step, 0)

            def turn_step(k, carry):
                at = pl.ds(pl.multiple_of(k * 128, 128), 128)
                centred = tbuf[at, :].T - 1.5
                het = jnp.abs(centred) < 1.0
                zero = jnp.zeros_like(centred)
                out = pl.ds(b * 128, 128)
                lhs[0, out, at] = jnp.clip(jnp.where(het, zero, centred), -1.0, 1.0)
                lhs[1, out, at] = jnp.where(het, centred * -2.0, zero)
                lhs[2, out, at] = jnp.where(het, jnp.ones_like(centred), zero)
                return carry

            lax.fori_loop(0, samples // 128, turn_step, 0)

    def matmul(p, i):
        def col_step(n, carry):
            cols = pl.ds(pl.multiple_of(n * LANES, LANES), LANES)
            res = jnp.dot(lhs[p], feats[p, :, cols], preferred_element_type=F32)
            acc[p, i, :, :, :, cols] = res.reshape(2, 2, rows, LANES)
            return carry

        lax.fori_loop(0, genes // LANES, col_step, 0)
        for t in range(2):
            s0(p, i, t).start()

    def tile_step(i, carry):
        unpack(i)

        @pl.when(i > 0)
        def _():
            s0_then_s1(0, i - 1)

        matmul(1, i)

        @pl.when(i == 0)
        def _():
            marg_finish(0)
            marg_copy(1).start()

        matmul(2, i)
        s0_then_s1(1, i)
        matmul(0, i)
        s0_then_s1(2, i)
        return carry

    lax.fori_loop(0, 4, tile_step, 0)
    s0_then_s1(0, 3)
    marg_finish(1)
    marg_copy(2).start()

    def s2_total(k):
        return send(acc.at[0, k, y, c], r2.at[0, k], s2s.at[0, k], s2r.at[0, k], a_dev)

    def s2_allelic(k):
        t = oy if k == 0 else y
        return send(acc.at[1, 2, t, c], r2.at[1, k], s2s.at[1, k], s2r.at[1, k], b_dev)

    def s2_het(k):
        return send(acc.at[2, 1 + 2 * k, oy, c], r2.at[2, k], s2s.at[2, k], s2r.at[2, k], y_dev)

    def s3_total():
        return send(acc.at[0, 2, y, c], r3.at[0], s3s.at[0], s3r.at[0], b_dev)

    def s3_allelic():
        return send(acc.at[1, 3, oy, c], r3.at[1], s3s.at[1], s3r.at[1], y_dev)

    def s3_het():
        return send(acc.at[2, 1, y, c], r3.at[2], s3s.at[2], s3r.at[2], a_dev)

    for t in range(2):
        s1_allelic(0, t).wait_recv()
        acc[1, 2, t, c] = acc[1, 2, t, c] + r1[1, t]
    s2_allelic(0).start()
    s2_allelic(1).start()
    for t in range(2):
        s1_het(0, t).wait_recv()
        acc[2, 1, t, c] = acc[2, 1, t, c] + r1[2, t]
    s2_het(0).start()
    for k in range(2):
        s1_total(k).wait_recv()
        acc[0, k, y, c] = acc[0, k, y, c] + r1[0, k]
        s2_total(k).start()
    for k in range(2, 4):
        s1_total(k).wait_recv()
        acc[0, k, y, c] = acc[0, k, y, c] + r1[0, k]
    for t in range(2):
        s1_het(2, t).wait_recv()
        acc[2, 3, t, c] = acc[2, 3, t, c] + r1[2, 2 + t]
    s2_het(1).start()
    for t in range(2):
        s1_allelic(1, t).wait_recv()
        acc[1, 3, t, c] = acc[1, 3, t, c] + r1[1, 2 + t]

    marg_finish(2)
    marg_copy(3).start()

    s2_allelic(0).wait_recv()
    acc[1, 3, oy, c] = acc[1, 3, oy, c] + r2[1, 0]
    s3_allelic().start()
    s2_het(0).wait_recv()
    acc[2, 1, y, c] = acc[2, 1, y, c] + r2[2, 0]
    s3_het().start()
    s2_total(0).wait_recv()
    acc[0, 2, y, c] = acc[0, 2, y, c] + r2[0, 0]
    s3_total().start()

    marg_finish(3)
    gene_sum = marg[4, 0:1, :]
    gene_sq = marg[4, 1:2, :]
    lane = lax.broadcasted_iota(jnp.int32, (rows, marg.shape[2]), 1)
    row = lax.broadcasted_iota(jnp.int32, (rows, marg.shape[2]), 0)
    mine = lane == row + rows * s
    dos_sum = jnp.sum(jnp.where(mine, marg[4, 2:3, :], 0.0), axis=1, keepdims=True)
    dos_sq = jnp.sum(jnp.where(mine, marg[4, 3:4, :], 0.0), axis=1, keepdims=True)
    n = sample_count
    dosage_var = dos_sq - dos_sum * dos_sum / n
    gene_var = gene_sq - gene_sum * gene_sum / n

    s2_allelic(1).wait_recv()
    s2_het(1).wait_recv()
    s2_total(1).wait_recv()
    s3_allelic().wait_recv()
    s3_het().wait_recv()
    allelic = acc[1, 3, y, c] + r2[1, 1] + r3[1]
    het_weight = acc[2, 3, y, c] + r2[2, 1] + r3[2]
    za_ref[...] = allelic / jnp.sqrt(het_weight + 1.0)
    s3_total().wait_recv()
    total = acc[0, 3, y, c] + r2[0, 1] + r3[0]
    covariance = total - dos_sum * (gene_sum / n)
    scale = jnp.sqrt((dosage_var + 1.0) * (gene_var + 1.0))
    zt_ref[...] = (n**0.5) * covariance / scale

    for k in range(1, n_var):
        hap_copy(k).wait_send()
    for k in range(4):
        marg_copy(k).wait_send()

    def drain(i, carry):
        for p in range(3):
            for t in range(2):
                s0(p, i, t).wait_send()
        s1_total(i).wait_send()
        return carry

    lax.fori_loop(0, 4, drain, 0)
    for i in range(2):
        for t in range(2):
            s1_allelic(i, t).wait_send()
            s1_het(2 * i, t).wait_send()
        s2_total(i).wait_send()
        s2_allelic(i).wait_send()
        s2_het(i).wait_send()
    s3_total().wait_send()
    s3_allelic().wait_send()
    s3_het().wait_send()


def per_device(sample_count, hap_words, total_counts, allele_one, allele_two):
    n_var = lax.axis_size("var")
    words, block = hap_words.shape[1:]
    samples, genes = total_counts.shape
    variants = block * n_var
    rows = variants // 16
    tile = variants // 4
    dma = pltpu.SemaphoreType.DMA
    out = jax.ShapeDtypeStruct((rows, genes), F32)
    return pl.pallas_call(
        functools.partial(kernel, n_var, float(sample_count)),
        out_shape=(out, out),
        in_specs=[pl.BlockSpec(memory_space=pl.ANY)] * 4,
        out_specs=(pl.BlockSpec(memory_space=pltpu.VMEM),) * 2,
        scratch_shapes=[
            pltpu.VMEM((n_var, 2, words, block), jnp.int32),
            pltpu.VMEM((3, samples, genes), BF16),
            pltpu.VMEM((SLOTS, 3, ROWS_IN, genes), jnp.int32),
            pltpu.VMEM((2, 8, genes), F32),
            pltpu.VMEM((samples, 128), BF16),
            pltpu.VMEM((3, tile, samples), BF16),
            pltpu.VMEM((3, 4, 2, 2, rows, genes), F32),
            pltpu.VMEM((3, 4, 2, rows, genes), F32),
            pltpu.VMEM((3, 4, rows, genes), F32),
            pltpu.VMEM((3, 2, rows, genes), F32),
            pltpu.VMEM((3, rows, genes), F32),
            pltpu.VMEM((5, 8, variants), F32),
            pltpu.VMEM((4, 8, variants), F32),
            dma((SLOTS, 3)),
            dma,
            dma((n_var,)),
            dma((n_var,)),
            dma((3, 4, 2)),
            dma((3, 4, 2)),
            dma((3, 4)),
            dma((3, 4)),
            dma((3, 2)),
            dma((3, 2)),
            dma((3,)),
            dma((3,)),
            dma((4,)),
            dma((4,)),
        ],
        compiler_params=pltpu.CompilerParams(
            collective_id=0,
            has_side_effects=True,
            vmem_limit_bytes=64_000_000,
        ),
    )(hap_words, total_counts, allele_one, allele_two)


def solution(mesh):
    in_specs = (P(None, "samp", "var"), P("samp", "var"), P("samp", "var"), P("samp", "var"))
    out_specs = (P("samp", "var"), P("samp", "var"))

    def whole(hap_words, total_counts, allele_one, allele_two):
        body = functools.partial(per_device, total_counts.shape[0])
        return jax.shard_map(
            body, mesh=mesh, in_specs=in_specs, out_specs=out_specs, check_vma=False
        )(hap_words, total_counts, allele_one, allele_two)

    return whole
```

time: 251 us -> 83.4 us (0.33)
  waiting for transfers between devices: 130 us -> 0 us
  Pallas kernels: 0 us -> 79.2 us
  blocking collectives: 30.8 us -> 0 us
  other arithmetic: 27 us -> 0 us
  matrix products: 25.6 us -> 0 us
  local copies, waits for them, and re-layouts: 21.3 us -> 3.34 us
  between operations: 14.1 us -> 0.64 us
    reduce_scatter x1 -> x0, waiting for transfers between devices: 130 us -> none  [per_device(): lax.psum_scatter(pair_sums, 'samp', scatter_dimension=1, tiled=True)]
    pallas_call x0 -> x1, Pallas kernels: none -> 79.2 us  [per_device(): pl.pallas_call(functools.partial(kernel, n_var, float(sample_count)), out...]
    all_to_all x2 -> x0, blocking collectives: 30.8 us -> none  [from_everyone(): return lax.all_to_all(copies, axis, split_axis=0, concat_axis=0, tiled=True)]
    dot_general x3 -> x0, matrix products: 25.6 us -> none  [the longest x1 9.8 us: per_device(): jnp.einsum('sv,sg->vg', phase_b, weighted_b, preferred_element_type=jnp.f...]
    convert_element_type x3 -> x0, local copies, waits for them, and re-layouts: 18.3 us -> none  [the longest x1 6.14 us: per_device(): dosage_b = (bit_table[0] + bit_table[1] - 1).astype(jnp.bfloat16)]
    reduce_sum x3 -> x0, other arithmetic: 10.7 us -> none  [the longest x1 6.57 us: per_device(): jnp.sum(log_total, axis=0)]
    another operation x3 -> x0, other arithmetic: 5.31 us -> none  [the longest x1 5.28 us: per_device(): pair_sums = jnp.stack([cross_total, cross_allelic, het_weight])]
    convert_element_type x1 -> x0, other arithmetic: 4.65 us -> none  [per_device(): phase_b = phase_int.astype(jnp.bfloat16)]
  transfers between devices with their start and end apart: 2 -> 0, of which waited for: 1 -> 0; matrix products, arithmetic and copies ran while one was open for 23% -> 0% of each run, Pallas kernels for 0% -> 0%
where the time goes in v1:
time: 83.4 us; the launch traced here: 83.2 us
  Pallas kernels  79.2 us (95%)
  local copies, waits for them, and re-layouts  3.34 us (4%)
    pallas_call x1, Pallas kernels, per_device(): pl.pallas_call(functools.partial(kernel, n_var, float(sample_count)), out...  79.2 us
    unnamed x2, local copies, waits for them, and re-layouts  3.34 us

profile of v1, /device:TPU:1, one launch (start us, length us, event | category | flops | bytes accessed | tf_op | source)
XLA Modules:
  0.0 83.2 jit_solution(10032837434865232055)
XLA Ops:
  0.6 79.2 %shard_map.59 = (f32[64,1024]{1,0:T(8,128)}, f32[64,1024]{1,0:T(8,128)}) custom-call(s32[2,64,128]{2,1,0:T(8,128)} %hap_ref.1, s32[1920,1024]{1,0:T(8,128)} %total_ref.1, s32[1920,1024]{1,0:T(8,128)} %one_ref.1, s32[1920,1024]{1,0:T(8,128)} %two_ref.1), custom_call_target="tpu_custom_call" | custom-call | tf_op jit(solution)/shard_map/pallas_call | solution.py:434
  79.8 1.7 %copy.8 = f32[64,1024]{1,0:T(8,128)} copy(f32[64,1024]{1,0:T(8,128)} %get-tuple-element.4) | data formatting | bytes 524288
  81.5 1.7 %copy.9 = f32[64,1024]{1,0:T(8,128)} copy(f32[64,1024]{1,0:T(8,128)} %get-tuple-element.5) | data formatting | bytes 524288

commit v2 on v1

--- a/solution.py
+++ b/solution.py
@@ -9,7 +9,9 @@
 
 BITS = 30
 ROWS_IN = 128
-SLOTS = 4
+SLOTS = 3
+TURN = 5
+EARLY = 3
 LANES = 256
 MESH = pl.DeviceIdType.MESH
 BF16 = jnp.bfloat16
@@ -93,8 +95,6 @@
         pl.semaphore_signal(
             barrier, inc=1, device_id=(s, (v + k) % n_var), device_id_type=MESH
         )
-    pl.semaphore_wait(barrier, 4 + n_var - 1)
-
     own = pltpu.make_async_copy(hap_ref, hall.at[v], hap_own)
     own.start()
 
@@ -117,9 +117,6 @@
             device_id=(s, (v + k) % n_var),
             device_id_type=MESH,
         )
-
-    for k in range(1, n_var):
-        hap_copy(k).start()
 
     gacc[...] = jnp.zeros_like(gacc)
 
@@ -155,11 +152,19 @@
         lax.fori_loop(0, ROWS_IN // 16, row_step, 0)
         return carry
 
-    lax.fori_loop(0, n_chunks, chunk_step, 0)
-
-    own.wait()
+    with jax.named_scope("features_a"):
+        lax.fori_loop(0, EARLY, chunk_step, 0)
+    with jax.named_scope("barrier"):
+        pl.semaphore_wait(barrier, 4 + n_var - 1)
     for k in range(1, n_var):
-        hap_arrival(k).wait_recv()
+        hap_copy(k).start()
+    with jax.named_scope("features_b"):
+        lax.fori_loop(EARLY, n_chunks, chunk_step, 0)
+
+    with jax.named_scope("hap_wait"):
+        own.wait()
+        for k in range(1, n_var):
+            hap_arrival(k).wait_recv()
 
     marg[0] = jnp.zeros_like(marg[0])
     marg[0, 0:1, :] = jnp.sum(gacc[0], axis=0, keepdims=True)
@@ -185,7 +190,8 @@
         )
 
     def marg_finish(k):
-        marg_copy(k).wait_recv()
+        with jax.named_scope("marg_wait"):
+            marg_copy(k).wait_recv()
         marg[k + 1] = marg[k] + mrecv[k]
 
     marg_copy(0).start()
@@ -200,45 +206,59 @@
             device_id_type=MESH,
         )
 
-    def s0(p, i, t):
-        return send(acc.at[p, i, t, oc], r0.at[p, i, t], s0s.at[p, i, t], s0r.at[p, i, t], core_dev)
-
-    def s0_finish(p, i):
+    half = genes // 2
+    halves = (pl.ds(0, half), pl.ds(half, half))
+    whole = (pl.ds(0, genes),)
+
+    def parts(i):
+        return halves if i == 0 else whole
+
+    def s0(p, i, t, h):
+        cols = parts(i)[h]
+        return send(
+            acc.at[p, i, t, oc, :, cols],
+            r0.at[p, i, t, :, cols],
+            s0s.at[p, i, t, h],
+            s0r.at[p, i, t, h],
+            core_dev,
+        )
+
+    def s1(p, i, t, h):
+        cols = parts(i)[h]
+        if p == 0:
+            src, slot, dev = (i, oy), i, y_dev
+        elif p == 1:
+            src, slot, dev = (i, t), 2 * i + t, a_dev
+        else:
+            src, slot, dev = (i, t), i + t, b_dev
+        return send(
+            acc.at[p, src[0], src[1], c, :, cols],
+            r1.at[p, slot, :, cols],
+            s1s.at[p, slot, h],
+            s1r.at[p, slot, h],
+            dev,
+        )
+
+    def s1_pieces(p, i):
+        if p == 0:
+            return (0,)
+        if p == 1:
+            return (0, 1) if i < 2 else ()
+        return (0, 1) if i % 2 == 0 else ()
+
+    def s0_finish(p, i, h=0):
+        cols = parts(i)[h]
         for t in range(2):
-            s0(p, i, t).wait_recv()
-            acc[p, i, t, c] = acc[p, i, t, c] + r0[p, i, t]
-
-    def s1_total(i):
-        return send(acc.at[0, i, oy, c], r1.at[0, i], s1s.at[0, i], s1r.at[0, i], y_dev)
-
-    def s1_allelic(i, t):
-        at = 2 * i + t
-        return send(acc.at[1, i, t, c], r1.at[1, at], s1s.at[1, at], s1r.at[1, at], a_dev)
-
-    def s1_het(i, t):
-        return send(acc.at[2, i, t, c], r1.at[2, i + t], s1s.at[2, i + t], s1r.at[2, i + t], b_dev)
-
-    def s0_then_s1(p, i):
-        s0_finish(p, i)
-        if p == 0:
-            s1_total(i).start()
-        elif p == 1:
-
-            @pl.when(i < 2)
-            def _():
-                for t in range(2):
-                    s1_allelic(i, t).start()
-        else:
-
-            @pl.when(i % 2 == 0)
-            def _():
-                for t in range(2):
-                    s1_het(i, t).start()
+            with jax.named_scope("s0_wait"):
+                s0(p, i, t, h).wait_recv()
+            acc[p, i, t, c, :, cols] += r0[p, i, t, :, cols]
+        for t in s1_pieces(p, i):
+            s1(p, i, t, h).start()
 
     iota = lax.broadcasted_iota(jnp.int32, (8, 128), 0)
 
-    def unpack(i):
-        zt = jnp.where(i == 0, zc, jnp.where(i == 1, za, jnp.where(i == 2, zb, z)))
+    def unpack_words(i):
+        zt = (zc, za, zb, z)[i]
         for b in range(2):
             block = 2 * zt + b
 
@@ -261,59 +281,34 @@
                     code = ((u0 >> shift) & 1) | ((u1 >> shift) & 2)
                     parts.append(code.astype(F32))
                 out = pl.ds(pl.multiple_of(g * 8 * BITS, 16), 8 * BITS)
-                tbuf[out, :] = jnp.concatenate(parts, axis=0).astype(BF16)
+                tbuf[b, out, :] = jnp.concatenate(parts, axis=0).astype(BF16)
                 return carry
 
             lax.fori_loop(0, words // 8, word_step, 0)
 
-            def turn_step(k, carry):
-                at = pl.ds(pl.multiple_of(k * 128, 128), 128)
-                centred = tbuf[at, :].T - 1.5
-                het = jnp.abs(centred) < 1.0
-                zero = jnp.zeros_like(centred)
-                out = pl.ds(b * 128, 128)
-                lhs[0, out, at] = jnp.clip(jnp.where(het, zero, centred), -1.0, 1.0)
-                lhs[1, out, at] = jnp.where(het, centred * -2.0, zero)
-                lhs[2, out, at] = jnp.where(het, jnp.ones_like(centred), zero)
-                return carry
-
-            lax.fori_loop(0, samples // 128, turn_step, 0)
-
-    def matmul(p, i):
-        def col_step(n, carry):
-            cols = pl.ds(pl.multiple_of(n * LANES, LANES), LANES)
-            res = jnp.dot(lhs[p], feats[p, :, cols], preferred_element_type=F32)
-            acc[p, i, :, :, :, cols] = res.reshape(2, 2, rows, LANES)
+    def turn(i):
+        def turn_step(k, carry):
+            for b in range(2):
+                for j in range(TURN):
+                    at = pl.ds(pl.multiple_of(k * (TURN * 128) + j * 128, 128), 128)
+                    centred = tbuf[b, at, :].T - 1.5
+                    het = jnp.abs(centred) < 1.0
+                    zero = jnp.zeros_like(centred)
+                    out = pl.ds(b * 128, 128)
+                    lhs[i, 0, out, at] = jnp.clip(jnp.where(het, zero, centred), -1.0, 1.0)
+                    lhs[i, 1, out, at] = jnp.where(het, centred * -2.0, zero)
+                    lhs[i, 2, out, at] = jnp.where(het, jnp.ones_like(centred), zero)
             return carry
 
-        lax.fori_loop(0, genes // LANES, col_step, 0)
+        lax.fori_loop(0, samples // (TURN * 128), turn_step, 0)
+
+    def matmul(p, i, h=0):
+        cols = parts(i)[h]
+        with jax.named_scope("matmul"):
+            res = jnp.dot(lhs[i, p], feats[p, :, cols], preferred_element_type=F32)
+            acc[p, i, :, :, :, cols] = res.reshape(2, 2, rows, res.shape[1])
         for t in range(2):
-            s0(p, i, t).start()
-
-    def tile_step(i, carry):
-        unpack(i)
-
-        @pl.when(i > 0)
-        def _():
-            s0_then_s1(0, i - 1)
-
-        matmul(1, i)
-
-        @pl.when(i == 0)
-        def _():
-            marg_finish(0)
-            marg_copy(1).start()
-
-        matmul(2, i)
-        s0_then_s1(1, i)
-        matmul(0, i)
-        s0_then_s1(2, i)
-        return carry
-
-    lax.fori_loop(0, 4, tile_step, 0)
-    s0_then_s1(0, 3)
-    marg_finish(1)
-    marg_copy(2).start()
+            s0(p, i, t, h).start()
 
     def s2_total(k):
         return send(acc.at[0, k, y, c], r2.at[0, k], s2s.at[0, k], s2r.at[0, k], a_dev)
@@ -334,42 +329,103 @@
     def s3_het():
         return send(acc.at[2, 1, y, c], r3.at[2], s3s.at[2], s3r.at[2], a_dev)
 
-    for t in range(2):
-        s1_allelic(0, t).wait_recv()
-        acc[1, 2, t, c] = acc[1, 2, t, c] + r1[1, t]
+    def s1_recv(p, i, t):
+        for h in range(len(parts(i))):
+            with jax.named_scope(f"s1_{p}"):
+                s1(p, i, t, h).wait_recv()
+
+    def add_allelic(tile, k):
+        for t in range(2):
+            s1_recv(1, k, t)
+            acc[1, tile, t, c] = acc[1, tile, t, c] + r1[1, 2 * k + t]
+
+    def add_het(tile, k):
+        for t in range(2):
+            s1_recv(2, k, t)
+            acc[2, tile, t, c] = acc[2, tile, t, c] + r1[2, k + t]
+
+    def add_total(k):
+        s1_recv(0, k, 0)
+        acc[0, k, y, c] = acc[0, k, y, c] + r1[0, k]
+
+    def words_of(i):
+        with jax.named_scope("words"):
+            unpack_words(i)
+
+    def turn_of(i):
+        with jax.named_scope("turn"):
+            turn(i)
+
+    words_of(0)
+    turn_of(0)
+    matmul(0, 0, 0)
+    matmul(1, 0, 0)
+    marg_finish(0)
+    marg_copy(1).start()
+    matmul(2, 0, 0)
+    s0_finish(0, 0, 0)
+    matmul(0, 0, 1)
+    s0_finish(1, 0, 0)
+    marg_finish(1)
+    marg_copy(2).start()
+    matmul(1, 0, 1)
+    s0_finish(2, 0, 0)
+    matmul(2, 0, 1)
+    s0_finish(0, 0, 1)
+    words_of(1)
+    s0_finish(1, 0, 1)
+    turn_of(1)
+    s0_finish(2, 0, 1)
+    matmul(0, 1)
+    matmul(1, 1)
+    s0_finish(0, 1)
+    words_of(2)
+    s0_finish(1, 1)
+    turn_of(2)
+    marg_finish(2)
+    marg_copy(3).start()
+    matmul(2, 2)
+    matmul(0, 2)
+    s0_finish(2, 2)
+    words_of(3)
+    s0_finish(0, 2)
+    turn_of(3)
+    matmul(0, 3)
+    matmul(1, 2)
+    s0_finish(0, 3)
+    matmul(2, 1)
+    s0_finish(1, 2)
+    add_allelic(2, 0)
     s2_allelic(0).start()
     s2_allelic(1).start()
-    for t in range(2):
-        s1_het(0, t).wait_recv()
-        acc[2, 1, t, c] = acc[2, 1, t, c] + r1[2, t]
+    matmul(1, 3)
+    s0_finish(2, 1)
+    add_het(1, 0)
     s2_het(0).start()
-    for k in range(2):
-        s1_total(k).wait_recv()
-        acc[0, k, y, c] = acc[0, k, y, c] + r1[0, k]
-        s2_total(k).start()
-    for k in range(2, 4):
-        s1_total(k).wait_recv()
-        acc[0, k, y, c] = acc[0, k, y, c] + r1[0, k]
-    for t in range(2):
-        s1_het(2, t).wait_recv()
-        acc[2, 3, t, c] = acc[2, 3, t, c] + r1[2, 2 + t]
+    add_total(0)
+    s2_total(0).start()
+    matmul(2, 3)
+    s0_finish(1, 3)
+    add_total(1)
+    s2_total(1).start()
+    s0_finish(2, 3)
+    add_allelic(3, 1)
+    add_total(2)
+    add_het(3, 2)
     s2_het(1).start()
-    for t in range(2):
-        s1_allelic(1, t).wait_recv()
-        acc[1, 3, t, c] = acc[1, 3, t, c] + r1[1, 2 + t]
-
-    marg_finish(2)
-    marg_copy(3).start()
-
-    s2_allelic(0).wait_recv()
+    with jax.named_scope("s2_total"):
+        s2_total(0).wait_recv()
+    acc[0, 2, y, c] = acc[0, 2, y, c] + r2[0, 0]
+    s3_total().start()
+    with jax.named_scope("s2_allelic"):
+        s2_allelic(0).wait_recv()
     acc[1, 3, oy, c] = acc[1, 3, oy, c] + r2[1, 0]
     s3_allelic().start()
-    s2_het(0).wait_recv()
+    add_total(3)
+    with jax.named_scope("s2_het"):
+        s2_het(0).wait_recv()
     acc[2, 1, y, c] = acc[2, 1, y, c] + r2[2, 0]
     s3_het().start()
-    s2_total(0).wait_recv()
-    acc[0, 2, y, c] = acc[0, 2, y, c] + r2[0, 0]
-    s3_total().start()
 
     marg_finish(3)
     gene_sum = marg[4, 0:1, :]
@@ -383,15 +439,21 @@
     dosage_var = dos_sq - dos_sum * dos_sum / n
     gene_var = gene_sq - gene_sum * gene_sum / n
 
-    s2_allelic(1).wait_recv()
-    s2_het(1).wait_recv()
-    s2_total(1).wait_recv()
-    s3_allelic().wait_recv()
-    s3_het().wait_recv()
+    with jax.named_scope("s2_allelic"):
+        s2_allelic(1).wait_recv()
+    with jax.named_scope("s2_het"):
+        s2_het(1).wait_recv()
+    with jax.named_scope("s2_total"):
+        s2_total(1).wait_recv()
+    with jax.named_scope("s3_allelic"):
+        s3_allelic().wait_recv()
+    with jax.named_scope("s3_het"):
+        s3_het().wait_recv()
     allelic = acc[1, 3, y, c] + r2[1, 1] + r3[1]
     het_weight = acc[2, 3, y, c] + r2[2, 1] + r3[2]
     za_ref[...] = allelic / jnp.sqrt(het_weight + 1.0)
-    s3_total().wait_recv()
+    with jax.named_scope("s3_total"):
+        s3_total().wait_recv()
     total = acc[0, 3, y, c] + r2[0, 1] + r3[0]
     covariance = total - dos_sum * (gene_sum / n)
     scale = jnp.sqrt((dosage_var + 1.0) * (gene_var + 1.0))
@@ -402,18 +464,14 @@
     for k in range(4):
         marg_copy(k).wait_send()
 
-    def drain(i, carry):
+    for i in range(4):
         for p in range(3):
-            for t in range(2):
-                s0(p, i, t).wait_send()
-        s1_total(i).wait_send()
-        return carry
-
-    lax.fori_loop(0, 4, drain, 0)
+            for h in range(len(parts(i))):
+                for t in range(2):
+                    s0(p, i, t, h).wait_send()
+                for t in s1_pieces(p, i):
+                    s1(p, i, t, h).wait_send()
     for i in range(2):
-        for t in range(2):
-            s1_allelic(i, t).wait_send()
-            s1_het(2 * i, t).wait_send()
         s2_total(i).wait_send()
         s2_allelic(i).wait_send()
         s2_het(i).wait_send()
@@ -434,15 +492,15 @@
     return pl.pallas_call(
         functools.partial(kernel, n_var, float(sample_count)),
         out_shape=(out, out),
-        in_specs=[pl.BlockSpec(memory_space=pl.ANY)] * 4,
+        in_specs=[pl.BlockSpec(memory_space=pltpu.HBM)] * 4,
         out_specs=(pl.BlockSpec(memory_space=pltpu.VMEM),) * 2,
         scratch_shapes=[
             pltpu.VMEM((n_var, 2, words, block), jnp.int32),
             pltpu.VMEM((3, samples, genes), BF16),
             pltpu.VMEM((SLOTS, 3, ROWS_IN, genes), jnp.int32),
             pltpu.VMEM((2, 8, genes), F32),
-            pltpu.VMEM((samples, 128), BF16),
-            pltpu.VMEM((3, tile, samples), BF16),
+            pltpu.VMEM((2, samples, 128), BF16),
+            pltpu.VMEM((4, 3, tile, samples), BF16),
             pltpu.VMEM((3, 4, 2, 2, rows, genes), F32),
             pltpu.VMEM((3, 4, 2, rows, genes), F32),
             pltpu.VMEM((3, 4, rows, genes), F32),
@@ -454,10 +512,10 @@
             dma,
             dma((n_var,)),
             dma((n_var,)),
+            dma((3, 4, 2, 2)),
+            dma((3, 4, 2, 2)),
             dma((3, 4, 2)),
             dma((3, 4, 2)),
-            dma((3, 4)),
-            dma((3, 4)),
             dma((3, 2)),
             dma((3, 2)),
             dma((3,)),
@@ -468,7 +526,7 @@
         compiler_params=pltpu.CompilerParams(
             collective_id=0,
             has_side_effects=True,
-            vmem_limit_bytes=64_000_000,
+            vmem_limit_bytes=55_600_000,
         ),
     )(hap_words, total_counts, allele_one, allele_two)
 

time: 83.4 us -> 69.8 us (0.84)
  Pallas kernels: 79.2 us -> 66.7 us
  local copies, waits for them, and re-layouts: 3.34 us -> 2.24 us
    pallas_call x1, Pallas kernels: 79.2 us -> 66.7 us  [per_device(): pl.pallas_call(functools.partial(kernel, n_var, float(sample_count)), out...]
    unnamed x2 -> x4, local copies, waits for them, and re-layouts: 3.34 us -> 2.24 us
where the time goes in v2:
time: 69.8 us; the launch traced here: 69.6 us
  Pallas kernels  66.7 us (96%)
  local copies, waits for them, and re-layouts  2.24 us (3%)
    pallas_call x1, Pallas kernels, per_device(): pl.pallas_call(functools.partial(kernel, n_var, float(sample_count)), out...  66.7 us
    unnamed x4, local copies, waits for them, and re-layouts  2.24 us

profile of v2, /device:TPU:1, one launch (start us, length us, event | category | flops | bytes accessed | tf_op | source)
XLA Modules:
  0.0 69.6 jit_solution(14017314388646120164)
XLA Ops:
  0.6 0.0 copy-start
  0.6 0.8 %copy-done = s32[2,64,128]{2,1,0:T(8,128)S(1)} copy-done((s32[2,64,128]{2,1,0:T(8,128)S(1)}, s32[2,64,128]{2,1,0:T(8,128)}, u32[]{:S(2)}) %copy-start) | copy-done | bytes 65560
  1.5 66.7 %shard_map.59 = (f32[64,1024]{1,0:T(8,128)S(1)}, f32[64,1024]{1,0:T(8,128)S(1)}) custom-call(s32[2,64,128]{2,1,0:T(8,128)S(1)} %copy-done, s32[1920,1024]{1,0:T(8,128)} %total_ref.1, s32[1920,1024]{1,0:T(8,128)} %one_ref.1, s32[1920,1024]{1,0:T(8,128)} %two_ref.1), custom_call_target="tpu_custom_call" | custom-call | tf_op jit(solution)/shard_map/pallas_call | solution.py:492
  68.2 0.7 %copy.8 = f32[64,1024]{1,0:T(8,128)} copy(f32[64,1024]{1,0:T(8,128)S(1)} %get-tuple-element.4) | data formatting | bytes 524288
  68.9 0.7 %copy.9 = f32[64,1024]{1,0:T(8,128)} copy(f32[64,1024]{1,0:T(8,128)S(1)} %get-tuple-element.5) | data formatting | bytes 524288
Async XLA Ops:
  0.6 0.8 %copy-start = (s32[2,64,128]{2,1,0:T(8,128)S(1)}, s32[2,64,128]{2,1,0:T(8,128)}, u32[]{:S(2)}) copy-start(s32[2,64,128]{2,1,0:T(8,128)} %hap_ref.1) | copy-start | bytes 196612

commit v3 on v1

v3 whole, which is shorter than its diff:
```python
import functools

import jax
import jax.numpy as jnp
from jax import lax
from jax.experimental import pallas as pl
from jax.experimental.pallas import tpu as pltpu
from jax.sharding import PartitionSpec as P

BITS = 30
ROWS_IN = 128
SLOTS = 6
TURN = 5
DEFER = 2
STEP = 16
SEND_AT = (0, 4, 8, 12)
FAR_FIRST = (5, 4, 7, 6, 1, 3, 2)
LANES = 256
MESH = pl.DeviceIdType.MESH
BF16 = jnp.bfloat16
F32 = jnp.float32


def kernel(
    n_var,
    sample_count,
    hap_ref,
    total_ref,
    one_ref,
    two_ref,
    zt_ref,
    za_ref,
    hall,
    feats,
    gacc,
    acc,
    r0,
    r1,
    r2,
    r3,
    marg,
    mrecv,
    in_sem,
    hap_own,
    hap_send,
    hap_recv,
    s0s,
    s0r,
    s1s,
    s1r,
    s2s,
    s2r,
    s3s,
    s3r,
    ms,
    mr,
):
    samples, genes = total_ref.shape
    words = hap_ref.shape[1]
    rows = acc.shape[4]
    s = lax.axis_index("samp")
    v = lax.axis_index("var")
    c = s % 2
    y = (s // 2) % 2
    z = s // 4
    x = v // 2
    za = z + 1 - 2 * (z % 2)
    zb = 3 - z
    zc = (z + 2) % 4
    core_dev = (s + 1 - 2 * c, v)
    y_dev = (s + 2 - 4 * y, v)
    a_dev = (za * 4 + y * 2 + c, v)
    b_dev = (zb * 4 + y * 2 + c, v)
    chips = [((s + 2 * j) % 16, v) for j in range(1, 8)]
    oc = 1 - c
    oy = 1 - y

    half = genes // 2
    halves = (pl.ds(0, half), pl.ds(half, half))
    quarter = half // 2
    early = (pl.ds(0, quarter), pl.ds(quarter, quarter), halves[1])

    def pieces(i):
        return early if i == 0 else halves

    def pieces_of_half(i, h):
        return ((0, 1), (2,))[h] if i == 0 else (h,)

    n_chunks = samples // ROWS_IN

    def fetch(counts, k, slot, which, ref):
        at = pl.multiple_of(k * ROWS_IN, ROWS_IN)
        return pltpu.make_async_copy(
            ref.at[pl.ds(at, ROWS_IN), :],
            counts.at[slot, which],
            in_sem.at[slot],
        )

    sources = (total_ref, one_ref, two_ref)
    own = pltpu.make_async_copy(hap_ref, hall.at[v], hap_own)

    def peer(k, sign):
        return ((x + sign * (k // 2) + 4) % 4) * 2 + (v + k) % 2

    def hap_copy(k):
        return pltpu.make_async_remote_copy(
            src_ref=hap_ref,
            dst_ref=hall.at[v],
            send_sem=hap_send,
            recv_sem=hap_recv.at[k],
            device_id=(s, peer(k, 1)),
            device_id_type=MESH,
        )

    def hap_arrival(k):
        return pltpu.make_async_remote_copy(
            src_ref=hap_ref,
            dst_ref=hall.at[peer(k, -1)],
            send_sem=hap_send,
            recv_sem=hap_recv.at[k],
            device_id=(s, peer(k, 1)),
            device_id_type=MESH,
        )

    at_tile = [jnp.where(x == w, k, 0) for w, k in zip((zc, za, zb, z), SEND_AT)]
    send_at = sum(at_tile)

    gacc[...] = jnp.zeros_like(gacc)

    def chunk_step(counts, k, carry):
        slot = k % SLOTS

        @pl.when(k == send_at)
        def _():
            for m in FAR_FIRST:
                hap_copy(m).start()

        @pl.when(k + SLOTS - 1 < n_chunks)
        def _():
            for which, ref in enumerate(sources):
                fetch(counts, k + SLOTS - 1, (k + SLOTS - 1) % SLOTS, which, ref).start()

        pltpu.make_async_copy(counts.at[slot], counts.at[slot], in_sem.at[slot]).wait()
        def row_step(r, carry):
            at = pl.ds(pl.multiple_of(r * STEP, STEP), STEP)
            out = pl.ds(pl.multiple_of(k * ROWS_IN + r * STEP, STEP), STEP)
            for lane in range(0, genes, LANES):
                cols = pl.ds(lane, LANES)
                log_total = jnp.log((counts[slot, 0, at, cols] + 1).astype(F32))
                one = (counts[slot, 1, at, cols] + 1).astype(F32)
                two = (counts[slot, 2, at, cols] + 1).astype(F32)
                weight = (one * two) / (one + two)
                weighted = weight * (jnp.log(one) - jnp.log(two))
                feats[0, out, cols] = log_total.astype(BF16)
                feats[1, out, cols] = weighted.astype(BF16)
                feats[2, out, cols] = weight.astype(BF16)
                square = log_total * log_total
                gacc[0, :, cols] += log_total[:8] + log_total[8:]
                gacc[1, :, cols] += square[:8] + square[8:]
            return carry

        lax.fori_loop(0, ROWS_IN // STEP, row_step, 0, unroll=2)
        return carry

    def features(counts):
        for k in range(SLOTS - 1):
            for which, ref in enumerate(sources):
                fetch(counts, k, k, which, ref).start()

        barrier = pltpu.get_barrier_semaphore()
        for dev in (core_dev, *chips):
            pl.semaphore_signal(barrier, inc=1, device_id=dev, device_id_type=MESH)
        for k in range(1, n_var):
            pl.semaphore_signal(
                barrier, inc=1, device_id=(s, (v + k) % n_var), device_id_type=MESH
            )
        own.start()
        with jax.named_scope("barrier"):
            pl.semaphore_wait(barrier, 8 + n_var - 1)
        step = functools.partial(chunk_step, counts)
        with jax.named_scope("features"):
            lax.fori_loop(0, n_chunks, step, 0)

    def hap_wait(i):
        target = (zc, za, zb, z)[i]
        with jax.named_scope("hap_wait"):
            for b in range(2):
                k = ((x + 4 - target) % 4) * 2 + (v + b) % 2

                @pl.when(k == 0)
                def _():
                    own.wait()

                @pl.when(k != 0)
                def _():
                    hap_arrival(k).wait_recv()

    def gene_margins():
        marg[0, 0, 0:1, :] = jnp.sum(gacc[0], axis=0, keepdims=True)
        marg[0, 0, 1:2, :] = jnp.sum(gacc[1], axis=0, keepdims=True)

    def variant_margins():
        for b in range(n_var):
            w0, w1 = hall[b, 0], hall[b, 1]
            bits = lax.population_count(w0) + lax.population_count(w1)
            het = lax.population_count(jnp.bitwise_xor(w0, w1))
            cols = pl.ds(b * 128, 128)
            bit_sum = jnp.sum(bits.astype(F32), axis=0, keepdims=True)
            het_sum = jnp.sum(het.astype(F32), axis=0, keepdims=True)
            marg[1, 0, 0:1, cols] = bit_sum - float(samples)
            marg[1, 0, 1:2, cols] = float(samples) - het_sum

    def marg_pair(w):
        return pltpu.make_async_remote_copy(
            src_ref=marg.at[w, 0],
            dst_ref=mrecv.at[w, 0],
            send_sem=ms,
            recv_sem=mr.at[w, 0],
            device_id=core_dev,
            device_id_type=MESH,
        )

    def marg_chip(w, j):
        return pltpu.make_async_remote_copy(
            src_ref=marg.at[w, 1],
            dst_ref=mrecv.at[w, j],
            send_sem=ms,
            recv_sem=mr.at[w, 1],
            device_id=chips[j - 1],
            device_id_type=MESH,
        )

    def marg_share(w):
        with jax.named_scope("marg_wait"):
            marg_pair(w).wait_recv()
        marg[w, 1] = marg[w, 0] + mrecv[w, 0]
        for j in range(1, 8):
            marg_chip(w, j).start()

    def marg_total(w):
        others = mrecv.at[w, pl.ds(1, 7)]
        with jax.named_scope("marg_wait"):
            pltpu.make_async_copy(others, others, mr.at[w, 1]).wait()
        total = marg[w, 1]
        for j in range(1, 8):
            total = total + mrecv[w, j]
        return total

    def send(src, dst, ss, rs, dev):
        return pltpu.make_async_remote_copy(
            src_ref=src,
            dst_ref=dst,
            send_sem=ss,
            recv_sem=rs,
            device_id=dev,
            device_id_type=MESH,
        )

    def at_piece(i, g):
        return g if i == 0 else 1 + 2 * i + g

    def s0(p, i, g):
        cols = pieces(i)[g]
        return send(
            acc.at[p, i, :, oc, :, cols],
            r0.at[p, i, :, :, cols],
            s0s,
            s0r.at[p, at_piece(i, g)],
            core_dev,
        )

    def s1(p, i, g):
        cols = pieces(i)[g]
        if p == 0:
            src, dst, dev = acc.at[p, i, oy, c, :, cols], r1.at[p, i, :, cols], y_dev
        else:
            dev = a_dev if p == 1 else b_dev
            first = 2 * i if p == 1 else i
            src, dst = acc.at[p, i, :, c, :, cols], r1.at[p, pl.ds(first, 2), :, cols]
        return send(src, dst, s1s, s1r.at[p, at_piece(i, g)], dev)

    def goes_on(p, i):
        return p == 0 or (i < 2 if p == 1 else i % 2 == 0)

    def s0_finish(p, i, g):
        cols = pieces(i)[g]
        with jax.named_scope("s0_wait"):
            s0(p, i, g).wait_recv()
        for t in range(2):
            acc[p, i, t, c, :, cols] += r0[p, i, t, :, cols]
        if goes_on(p, i):
            s1(p, i, g).start()

    iota = lax.broadcasted_iota(jnp.int32, (8, 128), 0)

    def unpack_words(tbuf, i):
        zt = (zc, za, zb, z)[i]
        for b in range(2):
            block = 2 * zt + b

            def word_step(g, carry):
                at = pl.ds(pl.multiple_of(g * 8, 8), 8)
                w0 = hall[block, 0, at, :]
                w1 = hall[block, 1, at, :] << 1
                parts = []
                for t in range(BITS):
                    first = 8 * t // BITS
                    last = (8 * t + 7) // BITS
                    shift = iota + (8 * t - BITS * first)
                    u0 = jnp.broadcast_to(w0[first : first + 1], (8, 128))
                    u1 = jnp.broadcast_to(w1[first : first + 1], (8, 128))
                    if last != first:
                        early = iota < BITS * last - 8 * t
                        shift = jnp.where(early, shift, shift - BITS)
                        u0 = jnp.where(early, u0, jnp.broadcast_to(w0[last : last + 1], (8, 128)))
                        u1 = jnp.where(early, u1, jnp.broadcast_to(w1[last : last + 1], (8, 128)))
                    code = ((u0 >> shift) & 1) | ((u1 >> shift) & 2)
                    parts.append(code.astype(F32))
                out = pl.ds(pl.multiple_of(g * 8 * BITS, 16), 8 * BITS)
                tbuf[b, out, :] = jnp.concatenate(parts, axis=0).astype(BF16)
                return carry

            lax.fori_loop(0, words // 8, word_step, 0)

    def turn(tbuf, lhs, i):
        def turn_step(k, carry):
            for b in range(2):
                for j in range(TURN):
                    at = pl.ds(pl.multiple_of(k * (TURN * 128) + j * 128, 128), 128)
                    centred = tbuf[b, at, :].T - 1.5
                    het = jnp.abs(centred) < 1.0
                    zero = jnp.zeros_like(centred)
                    out = pl.ds(b * 128, 128)
                    lhs[i, 0, out, at] = jnp.clip(jnp.where(het, zero, centred), -1.0, 1.0)
                    lhs[i, 1, out, at] = jnp.where(het, centred * -2.0, zero)
                    lhs[i, 2, out, at] = jnp.where(het, jnp.ones_like(centred), zero)
            return carry

        lax.fori_loop(0, samples // (TURN * 128), turn_step, 0)

    def matmul(lhs, p, i, h):
        cols = pieces(i)[h]
        with jax.named_scope("matmul"):
            res = jnp.dot(lhs[i, p], feats[p, :, cols], preferred_element_type=F32)
            acc[p, i, :, :, :, cols] = res.reshape(2, 2, rows, res.shape[1])
        s0(p, i, h).start()

    def s2(p, k, h):
        if p == 0:
            src, dev = (k, y), a_dev
        elif p == 1:
            src, dev = (2, oy if k == 0 else y), b_dev
        else:
            src, dev = (1 + 2 * k, oy), y_dev
        return send(
            acc.at[p, src[0], src[1], c, :, halves[h]],
            r2.at[p, k, :, halves[h]],
            s2s,
            s2r.at[p, k, h],
            dev,
        )

    def s3(p, h):
        src, dev = (((2, y), b_dev), ((3, oy), y_dev), ((1, y), a_dev))[p]
        return send(
            acc.at[p, src[0], src[1], c, :, halves[h]],
            r3.at[p, :, halves[h]],
            s3s,
            s3r.at[p, h],
            dev,
        )

    def s1_arrival(p, i, h):
        for g in pieces_of_half(i, h):
            with jax.named_scope(f"s1_{p}"):
                s1(p, i, g).wait_recv()

    def add_allelic(tile, k, h):
        s1_arrival(1, k, h)
        for t in range(2):
            acc[1, tile, t, c, :, halves[h]] += r1[1, 2 * k + t, :, halves[h]]

    def add_het(tile, k, h):
        s1_arrival(2, k, h)
        for t in range(2):
            acc[2, tile, t, c, :, halves[h]] += r1[2, k + t, :, halves[h]]

    def add_total(k, h):
        s1_arrival(0, k, h)
        acc[0, k, y, c, :, halves[h]] += r1[0, k, :, halves[h]]

    def pass_on(p, h):
        with jax.named_scope(f"s2_{p}_0"):
            s2(p, 0, h).wait_recv()
        tile, t = ((2, y), (3, oy), (1, y))[p]
        acc[p, tile, t, c, :, halves[h]] += r2[p, 0, :, halves[h]]
        s3(p, h).start()

    def last_add(p, h):
        with jax.named_scope(f"s2_{p}_1"):
            s2(p, 1, h).wait_recv()
        with jax.named_scope(f"s3_{p}"):
            s3(p, h).wait_recv()
        return acc[p, 3, y, c, :, halves[h]] + r2[p, 1, :, halves[h]] + r3[p, :, halves[h]]

    def all_sent(ref, sem):
        pltpu.make_async_copy(ref, ref, sem).wait()

    def drain_first():
        all_sent(hall.at[pl.ds(0, n_var - 1)], hap_send)
        all_sent(mrecv, ms)
        all_sent(r0, s0s)
        all_sent(r1, s1s)

    def products(tbuf, lhs):
        def words_of(i):
            hap_wait(i)
            with jax.named_scope("words"):
                unpack_words(tbuf, i)

        def turn_of(i):
            with jax.named_scope("turn"):
                turn(tbuf, lhs, i)

        pending = []

        def mm(*steps):
            for step in steps:
                matmul(lhs, *step)
                pending.append(step)
                if len(pending) > (DEFER if step[1] else DEFER + 1):
                    go_on(1)

        def go_on(count):
            for step in pending[:count]:
                s0_finish(*step)
            del pending[:count]

        words_of(0)
        marg_share(0)
        turn_of(0)
        for g in range(3):
            mm((0, 0, g), (1, 0, g), (2, 0, g))
        words_of(1)
        go_on(3)
        turn_of(1)
        mm((0, 1, 0), (0, 1, 1))
        words_of(2)
        go_on(2)
        turn_of(2)
        mm((0, 2, 0), (1, 1, 0), (2, 2, 0), (0, 2, 1))
        words_of(3)
        go_on(2)
        turn_of(3)
        variant_margins()
        marg_pair(1).start()
        mm((0, 3, 0), (1, 1, 1), (2, 2, 1), (0, 3, 1))
        marg_share(1)
        mm((1, 2, 0), (2, 1, 0), (1, 2, 1), (2, 1, 1))
        add_allelic(2, 0, 0)
        s2(1, 0, 0).start()
        add_total(0, 0)
        s2(0, 0, 0).start()
        mm((2, 3, 0),)
        add_het(1, 0, 0)
        s2(2, 0, 0).start()
        add_total(0, 1)
        s2(0, 0, 1).start()
        mm((1, 3, 0))
        add_allelic(2, 0, 1)
        for k, h in ((0, 1), (1, 0), (1, 1)):
            s2(1, k, h).start()
        mm((2, 3, 1))
        add_het(1, 0, 1)
        s2(2, 0, 1).start()
        mm((1, 3, 1))
        go_on(len(pending))

    variants = n_var * 128
    pl.run_scoped(features, pltpu.VMEM((SLOTS, 3, ROWS_IN, genes), jnp.int32))
    gene_margins()
    marg_pair(0).start()
    pl.run_scoped(
        products,
        pltpu.VMEM((2, samples, 128), BF16),
        pltpu.VMEM((4, 3, variants // 4, samples), BF16),
    )
    for h in range(2):
        add_total(1, h)
        s2(0, 1, h).start()
    add_het(3, 2, 0)
    s2(2, 1, 0).start()
    add_allelic(3, 1, 0)
    add_total(2, 0)
    add_total(2, 1)
    add_allelic(3, 1, 1)
    add_total(3, 0)
    add_het(3, 2, 1)
    s2(2, 1, 1).start()
    add_total(3, 1)
    for p in (2, 0, 1):
        pass_on(p, 0)
    for p in (2, 0, 1):
        pass_on(p, 1)

    gene_total = marg_total(0)
    variant_total = marg_total(1)
    gene_sum = gene_total[0:1]
    gene_sq = gene_total[1:2]
    lane = lax.broadcasted_iota(jnp.int32, (rows, marg.shape[3]), 1)
    row = lax.broadcasted_iota(jnp.int32, (rows, marg.shape[3]), 0)
    mine = lane == row + rows * s
    dos_sum = jnp.sum(jnp.where(mine, variant_total[0:1], 0.0), axis=1, keepdims=True)
    dos_sq = jnp.sum(jnp.where(mine, variant_total[1:2], 0.0), axis=1, keepdims=True)
    n = sample_count
    dosage_var = dos_sq - dos_sum * dos_sum / n
    gene_var = gene_sq - gene_sum * gene_sum / n
    with jax.named_scope("drain_first"):
        drain_first()
    mean = gene_sum / n
    scale = (n**0.5) / jnp.sqrt((dosage_var + 1.0) * (gene_var + 1.0))
    for h in range(2):
        cols = halves[h]
        allelic = last_add(1, h)
        het_weight = last_add(2, h)
        with jax.named_scope("fin_a"):
            za_ref[:, cols] = allelic / jnp.sqrt(het_weight + 1.0)
        if h == 1:
            all_sent(r2, s2s)
        total = last_add(0, h)
        at = slice(h * half, (h + 1) * half)
        with jax.named_scope("fin_t"):
            zt_ref[:, cols] = (total - dos_sum * mean[:, at]) * scale[:, at]

    with jax.named_scope("drain"):
        all_sent(r3, s3s)


def per_device(sample_count, hap_words, total_counts, allele_one, allele_two):
    n_var = lax.axis_size("var")
    words, block = hap_words.shape[1:]
    samples, genes = total_counts.shape
    variants = block * n_var
    rows = variants // 16
    dma = pltpu.SemaphoreType.DMA
    out = jax.ShapeDtypeStruct((rows, genes), F32)
    return pl.pallas_call(
        functools.partial(kernel, n_var, float(sample_count)),
        out_shape=(out, out),
        in_specs=[pl.BlockSpec(memory_space=pltpu.HBM)] * 4,
        out_specs=(pl.BlockSpec(memory_space=pltpu.VMEM),) * 2,
        scratch_shapes=[
            pltpu.VMEM((n_var, 2, words, block), jnp.int32),
            pltpu.VMEM((3, samples, genes), BF16),
            pltpu.VMEM((2, 8, genes), F32),
            pltpu.VMEM((3, 4, 2, 2, rows, genes), F32),
            pltpu.VMEM((3, 4, 2, rows, genes), F32),
            pltpu.VMEM((3, 4, rows, genes), F32),
            pltpu.VMEM((3, 2, rows, genes), F32),
            pltpu.VMEM((3, rows, genes), F32),
            pltpu.VMEM((2, 2, 2, variants), F32),
            pltpu.VMEM((2, 8, 2, variants), F32),
            dma((SLOTS,)),
            dma,
            dma,
            dma((n_var,)),
            dma,
            dma((3, 9)),
            dma,
            dma((3, 9)),
            dma,
            dma((3, 2, 2)),
            dma,
            dma((3, 2)),
            dma,
            dma((2, 2)),
        ],
        compiler_params=pltpu.CompilerParams(
            collective_id=0,
            has_side_effects=True,
            vmem_limit_bytes=55_600_000,
        ),
    )(hap_words, total_counts, allele_one, allele_two)


def solution(mesh):
    in_specs = (P(None, "samp", "var"), P("samp", "var"), P("samp", "var"), P("samp", "var"))
    out_specs = (P("samp", "var"), P("samp", "var"))

    def whole(hap_words, total_counts, allele_one, allele_two):
        body = functools.partial(per_device, total_counts.shape[0])
        return jax.shard_map(
            body, mesh=mesh, in_specs=in_specs, out_specs=out_specs, check_vma=False
        )(hap_words, total_counts, allele_one, allele_two)

    return whole
```

time: 83.4 us -> 68.4 us (0.82)
  Pallas kernels: 79.2 us -> 65.3 us
  local copies, waits for them, and re-layouts: 3.34 us -> 2.24 us
    pallas_call x1, Pallas kernels: 79.2 us -> 65.3 us  [per_device(): pl.pallas_call(functools.partial(kernel, n_var, float(sample_count)), out...]
    unnamed x2 -> x4, local copies, waits for them, and re-layouts: 3.34 us -> 2.24 us
where the time goes in v3:
time: 68.4 us; the launch traced here: 68.2 us
  Pallas kernels  65.3 us (95%)
  local copies, waits for them, and re-layouts  2.24 us (3%)
    pallas_call x1, Pallas kernels, per_device(): pl.pallas_call(functools.partial(kernel, n_var, float(sample_count)), out...  65.3 us
    unnamed x4, local copies, waits for them, and re-layouts  2.24 us

profile of v3, /device:TPU:1, one launch (start us, length us, event | category | flops | bytes accessed | tf_op | source)
XLA Modules:
  0.0 68.2 jit_solution(208943436059138279)
XLA Ops:
  0.6 0.0 copy-start
  0.6 0.8 %copy-done = s32[2,64,128]{2,1,0:T(8,128)S(1)} copy-done((s32[2,64,128]{2,1,0:T(8,128)S(1)}, s32[2,64,128]{2,1,0:T(8,128)}, u32[]{:S(2)}) %copy-start) | copy-done | bytes 65560
  1.5 65.3 %shard_map.59 = (f32[64,1024]{1,0:T(8,128)S(1)}, f32[64,1024]{1,0:T(8,128)S(1)}) custom-call(s32[2,64,128]{2,1,0:T(8,128)S(1)} %copy-done, s32[1920,1024]{1,0:T(8,128)} %total_ref.1, s32[1920,1024]{1,0:T(8,128)} %one_ref.1, s32[1920,1024]{1,0:T(8,128)} %two_ref.1), custom_call_target="tpu_custom_call" | custom-call | tf_op jit(solution)/shard_map/pallas_call | solution.py:547
  66.8 0.7 %copy.8 = f32[64,1024]{1,0:T(8,128)} copy(f32[64,1024]{1,0:T(8,128)S(1)} %get-tuple-element.4) | data formatting | bytes 524288
  67.5 0.7 %copy.9 = f32[64,1024]{1,0:T(8,128)} copy(f32[64,1024]{1,0:T(8,128)S(1)} %get-tuple-element.5) | data formatting | bytes 524288
Async XLA Ops:
  0.6 0.8 %copy-start = (s32[2,64,128]{2,1,0:T(8,128)S(1)}, s32[2,64,128]{2,1,0:T(8,128)}, u32[]{:S(2)}) copy-start(s32[2,64,128]{2,1,0:T(8,128)} %hap_ref.1) | copy-start | bytes 196612

commit v4 on v3

--- a/solution.py
+++ b/solution.py
@@ -77,14 +77,6 @@
 
     half = genes // 2
     halves = (pl.ds(0, half), pl.ds(half, half))
-    quarter = half // 2
-    early = (pl.ds(0, quarter), pl.ds(quarter, quarter), halves[1])
-
-    def pieces(i):
-        return early if i == 0 else halves
-
-    def pieces_of_half(i, h):
-        return ((0, 1), (2,))[h] if i == 0 else (h,)
 
     n_chunks = samples // ROWS_IN
 
@@ -256,34 +248,31 @@
             device_id_type=MESH,
         )
 
-    def at_piece(i, g):
-        return g if i == 0 else 1 + 2 * i + g
-
     def s0(p, i, g):
-        cols = pieces(i)[g]
+        cols = halves[g]
         return send(
             acc.at[p, i, :, oc, :, cols],
             r0.at[p, i, :, :, cols],
             s0s,
-            s0r.at[p, at_piece(i, g)],
+            s0r.at[p, 2 * i + g],
             core_dev,
         )
 
     def s1(p, i, g):
-        cols = pieces(i)[g]
+        cols = halves[g]
         if p == 0:
             src, dst, dev = acc.at[p, i, oy, c, :, cols], r1.at[p, i, :, cols], y_dev
         else:
             dev = a_dev if p == 1 else b_dev
             first = 2 * i if p == 1 else i
             src, dst = acc.at[p, i, :, c, :, cols], r1.at[p, pl.ds(first, 2), :, cols]
-        return send(src, dst, s1s, s1r.at[p, at_piece(i, g)], dev)
+        return send(src, dst, s1s, s1r.at[p, 2 * i + g], dev)
 
     def goes_on(p, i):
         return p == 0 or (i < 2 if p == 1 else i % 2 == 0)
 
     def s0_finish(p, i, g):
-        cols = pieces(i)[g]
+        cols = halves[g]
         with jax.named_scope("s0_wait"):
             s0(p, i, g).wait_recv()
         for t in range(2):
@@ -339,7 +328,7 @@
         lax.fori_loop(0, samples // (TURN * 128), turn_step, 0)
 
     def matmul(lhs, p, i, h):
-        cols = pieces(i)[h]
+        cols = halves[h]
         with jax.named_scope("matmul"):
             res = jnp.dot(lhs[i, p], feats[p, :, cols], preferred_element_type=F32)
             acc[p, i, :, :, :, cols] = res.reshape(2, 2, rows, res.shape[1])
@@ -371,9 +360,8 @@
         )
 
     def s1_arrival(p, i, h):
-        for g in pieces_of_half(i, h):
-            with jax.named_scope(f"s1_{p}"):
-                s1(p, i, g).wait_recv()
+        with jax.named_scope(f"s1_{p}"):
+            s1(p, i, h).wait_recv()
 
     def add_allelic(tile, k, h):
         s1_arrival(1, k, h)
@@ -428,7 +416,7 @@
             for step in steps:
                 matmul(lhs, *step)
                 pending.append(step)
-                if len(pending) > (DEFER if step[1] else DEFER + 1):
+                if len(pending) > DEFER:
                     go_on(1)
 
         def go_on(count):
@@ -439,10 +427,10 @@
         words_of(0)
         marg_share(0)
         turn_of(0)
-        for g in range(3):
+        for g in range(2):
             mm((0, 0, g), (1, 0, g), (2, 0, g))
         words_of(1)
-        go_on(3)
+        go_on(2)
         turn_of(1)
         mm((0, 1, 0), (0, 1, 1))
         words_of(2)
@@ -536,6 +524,17 @@
         all_sent(r3, s3s)
 
 
+def hand_over(zt_held, za_held, zt_ref, za_ref, sems):
+    copies = (
+        pltpu.make_async_copy(zt_held, zt_ref, sems.at[0]),
+        pltpu.make_async_copy(za_held, za_ref, sems.at[1]),
+    )
+    for copy in copies:
+        copy.start()
+    for copy in copies:
+        copy.wait()
+
+
 def per_device(sample_count, hap_words, total_counts, allele_one, allele_two):
     n_var = lax.axis_size("var")
     words, block = hap_words.shape[1:]
@@ -544,7 +543,7 @@
     rows = variants // 16
     dma = pltpu.SemaphoreType.DMA
     out = jax.ShapeDtypeStruct((rows, genes), F32)
-    return pl.pallas_call(
+    held = pl.pallas_call(
         functools.partial(kernel, n_var, float(sample_count)),
         out_shape=(out, out),
         in_specs=[pl.BlockSpec(memory_space=pltpu.HBM)] * 4,
@@ -565,9 +564,9 @@
             dma,
             dma((n_var,)),
             dma,
-            dma((3, 9)),
+            dma((3, 8)),
             dma,
-            dma((3, 9)),
+            dma((3, 8)),
             dma,
             dma((3, 2, 2)),
             dma,
@@ -580,7 +579,15 @@
             has_side_effects=True,
             vmem_limit_bytes=55_600_000,
         ),
-    )(hap_words, total_counts, allele_one, allele_two)
+    )(pltpu.with_memory_space_constraint(hap_words, pltpu.HBM), total_counts, allele_one, allele_two)
+    return pl.pallas_call(
+        hand_over,
+        out_shape=(out, out),
+        in_specs=[pl.BlockSpec(memory_space=pltpu.VMEM)] * 2,
+        out_specs=(pl.BlockSpec(memory_space=pltpu.HBM),) * 2,
+        scratch_shapes=[dma((2,))],
+        compiler_params=pltpu.CompilerParams(vmem_limit_bytes=2_000_000),
+    )(*held)
 
 
 def solution(mesh):

time: 68.4 us -> 66.5 us (0.972)
  local copies, waits for them, and re-layouts: 2.24 us -> 0 us
    unnamed x4 -> x0, local copies, waits for them, and re-layouts: 2.24 us -> none
    pallas_call x0 -> x1, Pallas kernels: none -> 0.81 us  [per_device(): pl.pallas_call(hand_over, out_shape=(out, out), in_specs=[pl.BlockSpec(me...]
where the time goes in v4:
time: 66.5 us; the launch traced here: 66.4 us
  Pallas kernels  65.6 us (99%)
  between operations  0.8 us (1%)
    pallas_call x1, Pallas kernels, per_device(): pl.pallas_call(functools.partial(kernel, n_var, float(sample_count)), out...  64.8 us

profile of v4, /device:TPU:1, one launch (start us, length us, event | category | flops | bytes accessed | tf_op | source)
XLA Modules:
  0.0 66.4 jit_solution(13829948060932134950)
XLA Ops:
  0.6 64.8 %shard_map.59 = (f32[64,1024]{1,0:T(8,128)S(1)}, f32[64,1024]{1,0:T(8,128)S(1)}) custom-call(s32[2,64,128]{2,1,0:T(8,128)} %hap_ref.1, s32[1920,1024]{1,0:T(8,128)} %total_ref.1, s32[1920,1024]{1,0:T(8,128)} %one_ref.1, s32[1920,1024]{1,0:T(8,128)} %two_ref.1), custom_call_target="tpu_custom_call" | custom-call | tf_op jit(solution)/shard_map/pallas_call | solution.py:546
  65.4 0.8 %shard_map.60 = (f32[64,1024]{1,0:T(8,128)}, f32[64,1024]{1,0:T(8,128)}) custom-call(f32[64,1024]{1,0:T(8,128)S(1)} %get-tuple-element.4.zt_held, f32[64,1024]{1,0:T(8,128)S(1)} %get-tuple-element.5.za_held), custom_call_target="tpu_custom_call" | custom-call | tf_op jit(solution)/shard_map/pallas_call | solution.py:583

commit v5 on v4

--- a/solution.py
+++ b/solution.py
@@ -151,14 +151,10 @@
                 gacc[1, :, cols] += square[:8] + square[8:]
             return carry
 
-        lax.fori_loop(0, ROWS_IN // STEP, row_step, 0, unroll=2)
+        lax.fori_loop(0, ROWS_IN // STEP, row_step, 0, unroll=8)
         return carry
 
     def features(counts):
-        for k in range(SLOTS - 1):
-            for which, ref in enumerate(sources):
-                fetch(counts, k, k, which, ref).start()
-
         barrier = pltpu.get_barrier_semaphore()
         for dev in (core_dev, *chips):
             pl.semaphore_signal(barrier, inc=1, device_id=dev, device_id_type=MESH)
@@ -166,6 +162,9 @@
             pl.semaphore_signal(
                 barrier, inc=1, device_id=(s, (v + k) % n_var), device_id_type=MESH
             )
+        for k in range(SLOTS - 1):
+            for which, ref in enumerate(sources):
+                fetch(counts, k, k, which, ref).start()
         own.start()
         with jax.named_scope("barrier"):
             pl.semaphore_wait(barrier, 8 + n_var - 1)

time: 66.5 us -> 65.6 us (0.986)
  Pallas kernels: 65.6 us -> 64.7 us
    pallas_call x1, Pallas kernels: 64.8 us -> 63.9 us  [per_device(): pl.pallas_call(functools.partial(kernel, n_var, float(sample_count)), out...]
where the time goes in v5:
time: 65.6 us; the launch traced here: 65.5 us
  Pallas kernels  64.7 us (99%)
  between operations  0.8 us (1%)
    pallas_call x1, Pallas kernels, per_device(): pl.pallas_call(functools.partial(kernel, n_var, float(sample_count)), out...  63.9 us

profile of v5, /device:TPU:1, one launch (start us, length us, event | category | flops | bytes accessed | tf_op | source)
XLA Modules:
  0.0 65.5 jit_solution(14514017083526207196)
XLA Ops:
  0.6 63.9 %shard_map.59 = (f32[64,1024]{1,0:T(8,128)S(1)}, f32[64,1024]{1,0:T(8,128)S(1)}) custom-call(s32[2,64,128]{2,1,0:T(8,128)} %hap_ref.1, s32[1920,1024]{1,0:T(8,128)} %total_ref.1, s32[1920,1024]{1,0:T(8,128)} %one_ref.1, s32[1920,1024]{1,0:T(8,128)} %two_ref.1), custom_call_target="tpu_custom_call" | custom-call | tf_op jit(solution)/shard_map/pallas_call | solution.py:545
  64.5 0.8 %shard_map.60 = (f32[64,1024]{1,0:T(8,128)}, f32[64,1024]{1,0:T(8,128)}) custom-call(f32[64,1024]{1,0:T(8,128)S(1)} %get-tuple-element.4.zt_held, f32[64,1024]{1,0:T(8,128)S(1)} %get-tuple-element.5.za_held), custom_call_target="tpu_custom_call" | custom-call | tf_op jit(solution)/shard_map/pallas_call | solution.py:582
